TPU v7x, 32 devices: a whole 2x2x4 slice. The times are simulated.
32 devices in a mesh: dp: 8 (over z, y), tensor: 4 (over x, core).
Axes of the slice: x: 2, y: 2, z: 4, core: 2. Of those that a mesh axis runs over, the one named last changes fastest.
Arguments:
- layer_outs: bfloat16 [5, 8192, 4096], P(None, 'dp', 'tensor'), may hold values from -6 to 6
- avg_grads: bfloat16 [4, 8192, 4096], P(None, 'dp', 'tensor'), may hold values from -0.0010299683 to 0.0010299683
- attn_mixed: bfloat16 [8192, 4096], P('dp', 'tensor'), may hold values from -96 to 96
- dwa_coefs: float32 [4, 5], replicated, may hold values from -1.5 to 1.5
Outputs:
- coef_grad: float32 [4, 5], replicated
- proj_grad: float32 [4096, 4096], P('dp', 'tensor')
All inputs are finite; a program needn't handle non-finite values.
Results may differ from a plain program's by a relative error of at most 0.0042.
Values may be sent and summed in bfloat16 or wider, within the bound.
A program may use at most 128 MiB of HBM per device.

v0:
```python
import jax
import jax.numpy as jnp
from jax import lax
from jax.sharding import PartitionSpec as P


def coef_partial(layer_outs, avg_grads):
    depth = avg_grads.shape[0]
    grads_flat = avg_grads.reshape(depth, -1)
    outs_flat = layer_outs.reshape(depth + 1, -1)
    return lax.dot_general(
        grads_flat, outs_flat, (((1,), (1,)), ((), ())), preferred_element_type=jnp.float32
    )


def coef_total(partial_sum):
    across = lax.psum(partial_sum, "tensor")
    return lax.psum(across, "dp")


def coef_masked(raw):
    depth = raw.shape[0]
    rows = jnp.arange(depth, dtype=jnp.int32)[:, None]
    cols = jnp.arange(depth + 1, dtype=jnp.int32)[None, :]
    return jnp.where(cols <= rows + 1, raw, jnp.float32(0.0))


def weight_grad(avg_grads, attn_mixed, dwa_coefs):
    depth = avg_grads.shape[0]
    first = dwa_coefs[depth - 2, depth - 1] * avg_grads[depth - 2].astype(jnp.float32)
    second = dwa_coefs[depth - 1, depth - 1] * avg_grads[depth - 1].astype(jnp.float32)
    out_grad = (first + second).astype(jnp.bfloat16)
    term = lax.dot_general(
        lax.all_gather(out_grad, "tensor", axis=1, tiled=True),
        attn_mixed,
        (((0,), (0,)), ((), ())),
        preferred_element_type=jnp.float32,
    )
    return lax.psum_scatter(term, "dp", scatter_dimension=0, tiled=True)


def local(layer_outs, avg_grads, attn_mixed, dwa_coefs):
    partial_sum = coef_partial(layer_outs, avg_grads)
    proj_grad = weight_grad(avg_grads, attn_mixed, dwa_coefs)
    raw = coef_total(partial_sum)
    return (coef_masked(raw), proj_grad)


def solution(mesh):
    in_specs = (P(None, "dp", "tensor"), P(None, "dp", "tensor"), P("dp", "tensor"), P())
    out_specs = (P(), P("dp", "tensor"))
    return jax.shard_map(local, mesh=mesh, in_specs=in_specs, out_specs=out_specs, check_vma=False)
```

profile of v0, /device:TPU:3, one launch (start us, length us, event | category | flops | bytes accessed | tf_op | source)
XLA Modules:
  0.0 375.8 jit_solution(9789960235942607915)
XLA Ops:
  7.2 0.0 copy-start
  7.2 0.0 all-gather.3.cloned.1.call-start
  7.2 1.5 fusion.11
  8.7 5.9 %add_convert_fusion = bf16[1,1024,1024]{2,1,0:T(8,128)(2,1)} fusion(bf16[4,1024,1024]{2,1,0:T(8,128)(2,1)} %param.5, f32[]{:T(128)} %bitcast.2, f32[]{:T(128)} %bitcast.1), kind=kLoop, calls=%fused_computation.5 | loop fusion | flops 6291456 | bytes 6291464 | tf_op jit(solution)/shard_map/convert_element_type | solution.py:32
  14.6 0.0 all-gather.3.cloned.1.call-update
  14.6 0.0 reduce-scatter.2.cloned.1.call-start
  14.7 58.9 %all-gather.3.cloned.1.call-done = bf16[1,1024,4096]{2,1,0:T(8,128)(2,1)} async-done(((bf16[1,1024,1024]{2,1,0:T(8,128)(2,1)}), bf16[1,1024,4096]{2,1,0:T(8,128)(2,1)}) %all-gather.3.cloned.1.call-update) | async-done | bytes 8388624 | tf_op jit(solution)/shard_map/all_gather | solution.py:34
  73.6 0.0 copy-done
  73.6 14.6 %fusion.2 = f32[4096,1024]{1,0:T(8,128)} fusion(bf16[1024,1024]{1,0:T(8,128)(2,1)S(1)} %copy-done, bf16[1,1024,4096]{2,1,0:T(8,128)(2,1)} %all-gather.3.cloned.1.call-done), kind=kOutput, calls=%fused_computation.2 | convolution fusion | flops 8589934592 | bytes 27262976 | tf_op jit(solution)/shard_map/dot_general | solution.py:33
  88.1 0.0 reduce-scatter.2.cloned.1.call-update
  88.2 28.5 %fusion.5 = f32[4,5]{1,0:T(4,128)S(1)} fusion(bf16[5,1024,1024]{2,1,0:T(8,128)(2,1)} %param.4, bf16[4,1024,1024]{2,1,0:T(8,128)(2,1)} %param.5), kind=kOutput, calls=%fused_computation.6 | convolution fusion | flops 41943040 | bytes 18874448 | tf_op jit(solution)/shard_map/dot_general | solution.py:11
  116.6 5.6 %psum.14 = f32[4,5]{1,0:T(4,128)S(1)} all-reduce(f32[4,5]{1,0:T(4,128)S(1)} %fusion.5), channel_id=1, replica_groups=mesh['dp'=8,'tensor'=4] {'tensor'}, use_global_device_ids=true, to_apply=%region_0.0 | all-reduce | flops 20 | bytes 160 | tf_op jit(solution)/shard_map/psum | solution.py:17
  122.2 19.0 %psum.15 = f32[4,5]{1,0:T(4,128)S(1)} all-reduce(f32[4,5]{1,0:T(4,128)S(1)} %psum.14), channel_id=1, replica_groups=mesh['dp'=8,'tensor'=4] {'dp'}, use_global_device_ids=true, to_apply=%region_1.0 | all-reduce | flops 20 | bytes 160 | tf_op jit(solution)/shard_map/psum | solution.py:18
  141.2 0.7 fusion.10
  141.8 227.2 %reduce-scatter.2.cloned.1.call-done = f32[512,1024]{1,0:T(8,128)} async-done(((f32[4096,1024]{1,0:T(8,128)}), f32[512,1024]{1,0:T(8,128)}) %reduce-scatter.2.cloned.1.call-update) | async-done | bytes 2097168 | tf_op jit(solution)/shard_map/reduce_scatter | solution.py:39
  (1 shorter events, 0.0 us)
Async XLA Ops:
  7.2 66.4 %copy-start = (bf16[1024,1024]{1,0:T(8,128)(2,1)S(1)}, bf16[1024,1024]{1,0:T(8,128)(2,1)}, u32[]{:S(2)}) copy-start(bf16[1024,1024]{1,0:T(8,128)(2,1)} %param.6) | copy-start | bytes 6291460
  7.2 66.4 %all-gather.3.cloned.1.call-start = ((), (), s32[]{:S(2)}) async-start(), calls=%async_computation.2 | async-start | bytes 10485760 | tf_op jit(solution)/shard_map/all_gather | solution.py:34
  14.6 354.4 %reduce-scatter.2.cloned.1.call-start = ((), (), s32[]{:S(2)}) async-start(), calls=%async_computation.1 | async-start | bytes 18874368 | tf_op jit(solution)/shard_map/reduce_scatter | solution.py:39
Sparse Core Ops, SparseCore 0:
  14.8 58.7 all-gather.2
  88.3 280.6 reduce-scatter.1
where the time goes:
time: 378 us; the launch traced here: 376 us
  waiting for transfers between devices  286 us (76%)
  matrix products  43 us (11%)
  blocking collectives  24.6 us (7%)
  between operations  14 us (4%)
  other arithmetic  6.55 us (2%)
    reduce_scatter x1, waiting for transfers between devices, weight_grad(): return lax.psum_scatter(term, 'dp', scatter_dimension=0, tiled=True)  227 us
    all_gather x1, waiting for transfers between devices, weight_grad(): lax.all_gather(out_grad, 'tensor', axis=1, tiled=True)  58.9 us
    dot_general x1, matrix products, coef_partial(): lax.dot_general(grads_flat, outs_flat, (((1,), (1,)), ((), ())), preferre...  28.5 us
    psum x1, blocking collectives, coef_total(): return lax.psum(across, 'dp')  19 us
    dot_general x1, matrix products, weight_grad(): lax.dot_general(lax.all_gather(out_grad, 'tensor', axis=1, tiled=True), a...  14.6 us
  transfers between devices with their start and end apart: 2, of which 2 were waited for; matrix products, arithmetic and copies ran while one was open for 8% of the time, Pallas kernels for 0%

commit v1 on v0

v1 whole, which is shorter than its diff:
```python
import functools

import jax
import jax.numpy as jnp
from jax import lax
from jax.experimental import pallas as pl
from jax.experimental.pallas import tpu as pltpu
from jax.sharding import PartitionSpec as P

CHUNKS = 4
LANES = 128


def kernel(
    dp_size, tensor_size, outs_hbm, grads_hbm, attn_hbm, coefs, coef_out, proj_out,
    outs, grads, attn, gathered, y_send, y_recv, own, z_left, z_right, coef_a, coef_b,
    load_sem, g_send, x_send, g_recv, y_send_sem, y_recv_sem,
    z_send_sem, zl_sem, zr_sem, ca_send, ca_recv, cb_send, cb_recv,
):
    depth, tokens, features = grads.shape
    rows, cols = proj_out.shape
    ys = dp_size // tensor_size
    zs = tensor_size
    xs = tensor_size // 2
    chunk = rows // CHUNKS
    dp, tensor = lax.axis_index("dp"), lax.axis_index("tensor")
    z, y = dp // ys, dp % ys
    x, core = tensor // 2, tensor % 2
    partner = x * 2 + 1 - core

    loads = []
    order = [depth - 2, depth - 1]
    for i in order:
        loads.append(pltpu.make_async_copy(grads_hbm.at[i], grads.at[i], load_sem.at[i]))
    loads.append(pltpu.make_async_copy(attn_hbm, attn, load_sem.at[depth]))
    for i in range(depth - 2):
        loads.append(pltpu.make_async_copy(grads_hbm.at[i], grads.at[i], load_sem.at[i]))
    for j in range(depth + 1):
        loads.append(pltpu.make_async_copy(outs_hbm.at[j], outs.at[j], load_sem.at[depth + 1 + j]))
    for load in loads:
        load.start()

    barrier = pltpu.get_barrier_semaphore()
    for i in range(1, tensor_size):
        pl.semaphore_signal(
            barrier, inc=1, device_id={"tensor": (tensor + i) % tensor_size},
            device_id_type=pl.DeviceIdType.MESH,
        )
    for i in range(1, dp_size):
        pl.semaphore_signal(
            barrier, inc=1, device_id={"dp": (dp + i) % dp_size},
            device_id_type=pl.DeviceIdType.MESH,
        )
    pl.semaphore_wait(barrier, tensor_size + dp_size - 2)

    def piece(slot, part):
        return gathered.at[slot, pl.ds(pl.multiple_of(part * rows, rows), rows), :]

    def to_partner(slot, part):
        return pltpu.make_async_remote_copy(
            src_ref=piece(slot, part), dst_ref=piece(slot, part),
            send_sem=g_send.at[slot // 2, part], recv_sem=g_recv.at[slot, part],
            device_id={"tensor": partner}, device_id_type=pl.DeviceIdType.MESH,
        )

    def to_x(other, part):
        return pltpu.make_async_remote_copy(
            src_ref=piece(tensor, part), dst_ref=piece(tensor, part),
            send_sem=x_send.at[other, part], recv_sem=g_recv.at[tensor, part],
            device_id={"tensor": other * 2 + core}, device_id_type=pl.DeviceIdType.MESH,
        )

    def arrive(slot, part):
        pltpu.make_async_remote_copy(
            src_ref=piece(slot, part), dst_ref=piece(slot, part),
            send_sem=g_send.at[slot // 2, part], recv_sem=g_recv.at[slot, part],
            device_id={"tensor": partner}, device_id_type=pl.DeviceIdType.MESH,
        ).wait_recv()

    def make(part):
        first, second = coefs[depth - 2, depth - 1], coefs[depth - 1, depth - 1]

        @pl.loop(0, tokens // LANES)
        def _(step):
            at = pl.ds(pl.multiple_of(step * LANES, LANES), LANES)
            wide = pl.ds(pl.multiple_of(part * rows, LANES), rows)
            value = first * grads[depth - 2, at, wide].astype(jnp.float32)
            value += second * grads[depth - 1, at, wide].astype(jnp.float32)
            into = pl.ds(pl.multiple_of(part * rows, rows), rows)
            gathered[tensor, into, at] = value.T.astype(jnp.bfloat16)

        to_partner(tensor, part).start()
        for i in range(1, xs):
            to_x((x + i) % xs, part).start()

    def block(slot, part, k):
        at = pl.ds(pl.multiple_of(part * rows + k * chunk, chunk), chunk)
        return jnp.dot(gathered[slot, at, :], attn[...], preferred_element_type=jnp.float32)

    def strip(k):
        return pl.ds(pl.multiple_of(k * chunk, chunk), chunk)

    def y_copy(slot, i, k):
        return pltpu.make_async_remote_copy(
            src_ref=y_send.at[i - 1, slot, strip(k), :], dst_ref=y_recv.at[i - 1, slot, strip(k), :],
            send_sem=y_send_sem.at[i - 1, slot, k], recv_sem=y_recv_sem.at[i - 1, slot, k],
            device_id={"dp": z * ys + (y + i) % ys}, device_id_type=pl.DeviceIdType.MESH,
        )

    def y_start(slot):
        for i in range(1, ys):
            @pl.loop(0, CHUNKS)
            def _(k):
                y_send[i - 1, slot, strip(k), :] = block(slot, (y + i) % ys, k).astype(jnp.bfloat16)
                y_copy(slot, i, k).start()

    def keep(slot):
        @pl.loop(0, CHUNKS)
        def _(k):
            own[slot, strip(k), :] = block(slot, y, k)

    def right_copy(slot, k):
        return pltpu.make_async_remote_copy(
            src_ref=y_send.at[0, slot, strip(k), :], dst_ref=z_left.at[slot, strip(k), :],
            send_sem=z_send_sem.at[slot, k], recv_sem=zl_sem.at[slot, k],
            device_id={"dp": dp + ys}, device_id_type=pl.DeviceIdType.MESH,
        )

    def left_copy(slot, k):
        return pltpu.make_async_remote_copy(
            src_ref=y_send.at[0, slot, strip(k), :], dst_ref=z_right.at[slot, strip(k), :],
            send_sem=z_send_sem.at[slot, k], recv_sem=zr_sem.at[slot, k],
            device_id={"dp": dp - ys}, device_id_type=pl.DeviceIdType.MESH,
        )

    def pass_on(slot):
        @pl.loop(0, CHUNKS)
        def _(k):
            total = own[slot, strip(k), :]
            for i in range(1, ys):
                y_copy(slot, i, k).wait_send()
                y_copy(slot, i, k).wait_recv()
                total += y_recv[i - 1, slot, strip(k), :].astype(jnp.float32)
            own[slot, strip(k), :] = total

            @pl.when(slot > z)
            def _():
                @pl.when(z > 0)
                def _():
                    right_copy(slot, k).wait_recv()
                    own[slot, strip(k), :] += z_left[slot, strip(k), :].astype(jnp.float32)

                y_send[0, slot, strip(k), :] = own[slot, strip(k), :].astype(jnp.bfloat16)
                right_copy(slot, k).start()

            @pl.when(slot < z)
            def _():
                @pl.when(z < zs - 1)
                def _():
                    left_copy(slot, k).wait_recv()
                    own[slot, strip(k), :] += z_right[slot, strip(k), :].astype(jnp.float32)

                y_send[0, slot, strip(k), :] = own[slot, strip(k), :].astype(jnp.bfloat16)
                left_copy(slot, k).start()

    def coef_partial():
        pairs = [(i, j) for i in range(depth) for j in range(min(i + 2, depth + 1))]

        def step(r, sums):
            at = pl.ds(pl.multiple_of(r * 16, 16), 16)
            sums = list(sums)
            for col in range(features // LANES):
                lanes = slice(col * LANES, (col + 1) * LANES)
                g = [grads[i, at, lanes].astype(jnp.float32) for i in range(depth)]
                o = [outs[j, at, lanes].astype(jnp.float32) for j in range(depth + 1)]
                for n, (i, j) in enumerate(pairs):
                    product = g[i] * o[j]
                    sums[n] += product[:8] + product[8:]
            return tuple(sums)

        zero = jnp.zeros((8, LANES), jnp.float32)
        sums = lax.fori_loop(0, tokens // 16, step, tuple(zero for _ in pairs))
        row = lax.broadcasted_iota(jnp.int32, (8, LANES), 0)
        col = lax.broadcasted_iota(jnp.int32, (8, LANES), 1)
        tile = zero
        for n, (i, j) in enumerate(pairs):
            value = jnp.sum(sums[n], axis=(0, 1), keepdims=True)
            tile = jnp.where((row == i) & (col == j), value, tile)
        return tile

    def a_copy(i, slot):
        return pltpu.make_async_remote_copy(
            src_ref=coef_a.at[slot], dst_ref=coef_a.at[slot],
            send_sem=ca_send.at[i], recv_sem=ca_recv.at[slot],
            device_id={"tensor": (tensor + i) % tensor_size},
            device_id_type=pl.DeviceIdType.MESH,
        )

    def b_copy(i, slot):
        return pltpu.make_async_remote_copy(
            src_ref=coef_b.at[slot], dst_ref=coef_b.at[slot],
            send_sem=cb_send.at[i], recv_sem=cb_recv.at[slot],
            device_id={"dp": (dp + i) % dp_size}, device_id_type=pl.DeviceIdType.MESH,
        )

    loads[0].wait()
    loads[1].wait()
    for i in range(1, ys):
        make((y + i) % ys)
    loads[2].wait()
    y_start(tensor)
    make(y)
    for i in range(1, ys):
        arrive(partner, (y + i) % ys)
    y_start(partner)
    keep(tensor)
    arrive(partner, y)
    keep(partner)

    for load in loads[3:]:
        load.wait()
    coef_a[tensor] = coef_partial()
    for i in range(1, tensor_size):
        a_copy(i, tensor).start()

    for n in range(1, xs):
        other = (x + n) % xs
        for i in range(1, ys):
            arrive(other * 2 + core, (y + i) % ys)
            to_partner(other * 2 + core, (y + i) % ys).start()
        y_start(other * 2 + core)
        for i in range(1, ys):
            arrive(other * 2 + 1 - core, (y + i) % ys)
        y_start(other * 2 + 1 - core)

    pass_on(tensor)
    for i in range(1, tensor_size):
        a_copy(i, (tensor + tensor_size - i) % tensor_size).wait_recv()
    total = coef_a[0]
    for i in range(1, tensor_size):
        total += coef_a[i]
    coef_b[dp] = total
    for i in range(1, dp_size):
        b_copy(i, dp).start()
    pass_on(partner)

    for n in range(1, xs):
        other = (x + n) % xs
        arrive(other * 2 + core, y)
        to_partner(other * 2 + core, y).start()
        keep(other * 2 + core)
        arrive(other * 2 + 1 - core, y)
        keep(other * 2 + 1 - core)
        pass_on(other * 2 + core)
        pass_on(other * 2 + 1 - core)

    for i in range(1, dp_size):
        b_copy(i, (dp + dp_size - i) % dp_size).wait_recv()
    total = coef_b[0]
    for i in range(1, dp_size):
        total += coef_b[i]
    coef_out[...] = total[: coef_out.shape[0], : coef_out.shape[1]]

    @pl.loop(0, CHUNKS)
    def _(k):
        proj_out[strip(k), :] = own[z, strip(k), :]

        @pl.when(z > 0)
        def _():
            right_copy(z, k).wait_recv()
            proj_out[strip(k), :] += z_left[z, strip(k), :].astype(jnp.float32)

        @pl.when(z < zs - 1)
        def _():
            left_copy(z, k).wait_recv()
            proj_out[strip(k), :] += z_right[z, strip(k), :].astype(jnp.float32)

    for slot in range(zs):
        @pl.when(slot != z)
        def _():
            @pl.loop(0, CHUNKS)
            def _(k):
                right_copy(slot, k).wait_send()

    for part in range(ys):
        for n in range(xs):
            to_partner(n * 2 + core, part).wait_send()
        for n in range(1, xs):
            to_x((x + n) % xs, part).wait_send()
    for i in range(1, tensor_size):
        a_copy(i, tensor).wait_send()
    for i in range(1, dp_size):
        b_copy(i, dp).wait_send()


def local(dp_size, tensor_size, layer_outs, avg_grads, attn_mixed, dwa_coefs):
    depth, tokens, features = avg_grads.shape
    rows = features * tensor_size // dp_size
    cols = attn_mixed.shape[1]
    ys, zs, xs = dp_size // tensor_size, tensor_size, tensor_size // 2
    bf16, f32 = jnp.bfloat16, jnp.float32
    dma = pltpu.SemaphoreType.DMA
    any_space = pl.BlockSpec(memory_space=pl.ANY)
    vmem = pl.BlockSpec(memory_space=pltpu.VMEM)
    return pl.pallas_call(
        functools.partial(kernel, dp_size, tensor_size),
        out_shape=(
            jax.ShapeDtypeStruct(dwa_coefs.shape, f32),
            jax.ShapeDtypeStruct((rows, cols), f32),
        ),
        in_specs=[any_space, any_space, any_space, pl.BlockSpec(memory_space=pltpu.SMEM)],
        out_specs=(vmem, vmem),
        scratch_shapes=[
            pltpu.VMEM(layer_outs.shape, bf16),
            pltpu.VMEM(avg_grads.shape, bf16),
            pltpu.VMEM(attn_mixed.shape, bf16),
            pltpu.VMEM((tensor_size, features, tokens), bf16),
            pltpu.VMEM((ys - 1, zs, rows, cols), bf16),
            pltpu.VMEM((ys - 1, zs, rows, cols), bf16),
            pltpu.VMEM((zs, rows, cols), f32),
            pltpu.VMEM((zs, rows, cols), bf16),
            pltpu.VMEM((zs, rows, cols), bf16),
            pltpu.VMEM((tensor_size, 8, LANES), f32),
            pltpu.VMEM((dp_size, 8, LANES), f32),
            dma((2 * depth + 2,)),
            dma((xs, ys)),
            dma((xs, ys)),
            dma((tensor_size, ys)),
            dma((ys - 1, zs, CHUNKS)),
            dma((ys - 1, zs, CHUNKS)),
            dma((zs, CHUNKS)),
            dma((zs, CHUNKS)),
            dma((zs, CHUNKS)),
            dma((tensor_size,)),
            dma((tensor_size,)),
            dma((dp_size,)),
            dma((dp_size,)),
        ],
        compiler_params=pltpu.CompilerParams(
            collective_id=0, has_side_effects=True, vmem_limit_bytes=67000000
        ),
    )(layer_outs, avg_grads, attn_mixed, dwa_coefs)


def solution(mesh):
    sizes = (mesh.shape["dp"], mesh.shape["tensor"])
    in_specs = (P(None, "dp", "tensor"), P(None, "dp", "tensor"), P("dp", "tensor"), P())
    out_specs = (P(), P("dp", "tensor"))
    return jax.shard_map(
        functools.partial(local, *sizes), mesh=mesh, in_specs=in_specs, out_specs=out_specs, check_vma=False
    )
```

time: 378 us -> 155 us (0.41)
  waiting for transfers between devices: 286 us -> 0 us
  Pallas kernels: 0 us -> 149 us
  matrix products: 43 us -> 0 us
  blocking collectives: 24.6 us -> 0 us
  between operations: 14 us -> 0.64 us
  other arithmetic: 6.55 us -> 0 us
    reduce_scatter x1 -> x0, waiting for transfers between devices: 227 us -> none  [weight_grad(): return lax.psum_scatter(term, 'dp', scatter_dimension=0, tiled=True)]
    pallas_call x0 -> x1, Pallas kernels: none -> 149 us  [local(): pl.pallas_call(functools.partial(kernel, dp_size, tensor_size), out_shape...]
    all_gather x1 -> x0, waiting for transfers between devices: 58.9 us -> none  [weight_grad(): lax.all_gather(out_grad, 'tensor', axis=1, tiled=True)]
    dot_general x2 -> x0, matrix products: 43 us -> none  [the longest x1 28.5 us: coef_partial(): lax.dot_general(grads_flat, outs_flat, (((1,), (1,)), ((), ())), preferre...]
    psum x2 -> x0, blocking collectives: 24.6 us -> none  [the longest x1 19 us: coef_total(): return lax.psum(across, 'dp')]
    convert_element_type x1 -> x0, other arithmetic: 5.89 us -> none  [weight_grad(): out_grad = (first + second).astype(jnp.bfloat16)]
    unnamed x2, local copies, waits for them, and re-layouts: 0.01 us -> 4.4 us
  transfers between devices with their start and end apart: 2 -> 0, of which waited for: 2 -> 0; matrix products, arithmetic and copies ran while one was open for 8% -> 0% of each run, Pallas kernels for 0% -> 0%
where the time goes in v1:
time: 155 us; the launch traced here: 154 us
  Pallas kernels  149 us (96%)
  local copies, waits for them, and re-layouts  4.4 us (3%)
    pallas_call x1, Pallas kernels, local(): pl.pallas_call(functools.partial(kernel, dp_size, tensor_size), out_shape...  149 us
    unnamed x2, local copies, waits for them, and re-layouts  4.4 us

profile of v1, /device:TPU:3, one launch (start us, length us, event | category | flops | bytes accessed | tf_op | source)
XLA Modules:
  0.0 154.5 jit_solution(714287436812449252)
XLA Ops:
  0.6 149.4 %shard_map.59 = (f32[4,5]{1,0:T(4,128)}, f32[512,1024]{1,0:T(8,128)}) custom-call(bf16[5,1024,1024]{2,1,0:T(8,128)(2,1)} %outs_hbm.1, bf16[4,1024,1024]{2,1,0:T(8,128)(2,1)} %grads_hbm.1, bf16[1024,1024]{1,0:T(8,128)(2,1)} %attn_hbm.1, f32[4,5]{1,0:T(4,128)} %coefs.1), custom_call_target="tpu_custom_call" | custom-call | tf_op jit(solution)/shard_map/pallas_call | solution.py:305
  150.1 1.2 copy.8
  151.3 3.2 %copy.9 = f32[512,1024]{1,0:T(8,128)} copy(f32[512,1024]{1,0:T(8,128)} %get-tuple-element.5) | data formatting | bytes 4194304

commit v2 on v1

--- a/solution.py
+++ b/solution.py
@@ -7,7 +7,8 @@
 from jax.experimental.pallas import tpu as pltpu
 from jax.sharding import PartitionSpec as P
 
-CHUNKS = 4
+CHUNKS = 8
+GROUP = 4
 LANES = 128
 
 
@@ -37,7 +38,7 @@
         loads.append(pltpu.make_async_copy(grads_hbm.at[i], grads.at[i], load_sem.at[i]))
     for j in range(depth + 1):
         loads.append(pltpu.make_async_copy(outs_hbm.at[j], outs.at[j], load_sem.at[depth + 1 + j]))
-    for load in loads:
+    for load in loads[:3]:
         load.start()
 
     barrier = pltpu.get_barrier_semaphore()
@@ -94,11 +95,11 @@
             to_x((x + i) % xs, part).start()
 
     def block(slot, part, k):
-        at = pl.ds(pl.multiple_of(part * rows + k * chunk, chunk), chunk)
+        at = pl.ds(pl.multiple_of(part * rows + k * chunk, chunk), chunk * GROUP)
         return jnp.dot(gathered[slot, at, :], attn[...], preferred_element_type=jnp.float32)
 
-    def strip(k):
-        return pl.ds(pl.multiple_of(k * chunk, chunk), chunk)
+    def strip(k, count=1):
+        return pl.ds(pl.multiple_of(k * chunk, chunk), chunk * count)
 
     def y_copy(slot, i, k):
         return pltpu.make_async_remote_copy(
@@ -109,15 +110,19 @@
 
     def y_start(slot):
         for i in range(1, ys):
-            @pl.loop(0, CHUNKS)
-            def _(k):
-                y_send[i - 1, slot, strip(k), :] = block(slot, (y + i) % ys, k).astype(jnp.bfloat16)
-                y_copy(slot, i, k).start()
+            @pl.loop(0, CHUNKS // GROUP)
+            def _(g):
+                k = g * GROUP
+                value = block(slot, (y + i) % ys, k)
+                y_send[i - 1, slot, strip(k, GROUP), :] = value.astype(jnp.bfloat16)
+                for n in range(GROUP):
+                    y_copy(slot, i, k + n).start()
 
     def keep(slot):
-        @pl.loop(0, CHUNKS)
-        def _(k):
-            own[slot, strip(k), :] = block(slot, y, k)
+        @pl.loop(0, CHUNKS // GROUP)
+        def _(g):
+            k = g * GROUP
+            own[slot, strip(k, GROUP), :] = block(slot, y, k)
 
     def right_copy(slot, k):
         return pltpu.make_async_remote_copy(
@@ -209,6 +214,8 @@
         make((y + i) % ys)
     loads[2].wait()
     y_start(tensor)
+    for load in loads[3:]:
+        load.start()
     make(y)
     for i in range(1, ys):
         arrive(partner, (y + i) % ys)
@@ -223,15 +230,20 @@
     for i in range(1, tensor_size):
         a_copy(i, tensor).start()
 
+    others = []
     for n in range(1, xs):
         other = (x + n) % xs
+        far = jnp.where(other < xs // 2, other * 2, other * 2 + 1)
+        others.append((other, far, other * 4 + 1 - far))
+
+    for other, far, near in others:
         for i in range(1, ys):
             arrive(other * 2 + core, (y + i) % ys)
             to_partner(other * 2 + core, (y + i) % ys).start()
-        y_start(other * 2 + core)
         for i in range(1, ys):
             arrive(other * 2 + 1 - core, (y + i) % ys)
-        y_start(other * 2 + 1 - core)
+        y_start(far)
+        y_start(near)
 
     pass_on(tensor)
     for i in range(1, tensor_size):
@@ -242,17 +254,17 @@
     coef_b[dp] = total
     for i in range(1, dp_size):
         b_copy(i, dp).start()
-    pass_on(partner)
-
-    for n in range(1, xs):
-        other = (x + n) % xs
+
+    for other, far, near in others:
         arrive(other * 2 + core, y)
         to_partner(other * 2 + core, y).start()
-        keep(other * 2 + core)
         arrive(other * 2 + 1 - core, y)
-        keep(other * 2 + 1 - core)
-        pass_on(other * 2 + core)
-        pass_on(other * 2 + 1 - core)
+        keep(far)
+        keep(near)
+    pass_on(partner)
+    for other, far, near in others:
+        pass_on(far)
+        pass_on(near)
 
     for i in range(1, dp_size):
         b_copy(i, (dp + dp_size - i) % dp_size).wait_recv()

time: 155 us -> 142 us (0.916)
  the two profiles are of different devices: /device:TPU:3 before, /device:TPU:17 now
where the time goes in v2:
time: 142 us; the launch traced here: 141 us
  Pallas kernels  136 us (96%)
  local copies, waits for them, and re-layouts  4.4 us (3%)
    pallas_call x1, Pallas kernels, local(): pl.pallas_call(functools.partial(kernel, dp_size, tensor_size), out_shape...  136 us
    unnamed x2, local copies, waits for them, and re-layouts  4.4 us

profile of v2, /device:TPU:17, one launch (start us, length us, event | category | flops | bytes accessed | tf_op | source)
XLA Modules:
  0.0 141.4 jit_solution(8759425307819209105)
XLA Ops:
  0.6 136.4 %shard_map.59 = (f32[4,5]{1,0:T(4,128)}, f32[512,1024]{1,0:T(8,128)}) custom-call(bf16[5,1024,1024]{2,1,0:T(8,128)(2,1)} %outs_hbm.1, bf16[4,1024,1024]{2,1,0:T(8,128)(2,1)} %grads_hbm.1, bf16[1024,1024]{1,0:T(8,128)(2,1)} %attn_hbm.1, f32[4,5]{1,0:T(4,128)} %coefs.1), custom_call_target="tpu_custom_call" | custom-call | tf_op jit(solution)/shard_map/pallas_call | solution.py:317
  137.0 1.2 copy.8
  138.3 3.2 %copy.9 = f32[512,1024]{1,0:T(8,128)} copy(f32[512,1024]{1,0:T(8,128)} %get-tuple-element.5) | data formatting | bytes 4194304
